TPU v7x, 32 devices: a whole 2x2x4 slice. The times are simulated.
32 devices in a mesh: node: 16 (over z, y, core), local: 2 (over x).
Axes of the slice: x: 2, y: 2, z: 4, core: 2. Of those that a mesh axis runs over, the one named last changes fastest.
Arguments:
- tokens: bfloat16 [5120, 4096], P(('node', 'local')), may hold values from -6 to 6
- out_grad: bfloat16 [5120, 4096], P(('node', 'local')), may hold values from -6 to 6
- up_codes: bfloat16 [4096, 256], P('local'), may hold values from -127 to 127
- up_scales: float32 [4096, 2], P('local'), may hold values from 0.000109375 to 0.0004375
- down_codes: bfloat16 [4096, 256], P('local'), may hold values from -127 to 127
- down_scales: float32 [4096, 2], P('local'), may hold values from 0.000109375 to 0.0004375
Outputs:
- input_grad: bfloat16 [5120, 4096], P(('node', 'local'))
- grad_up: float32 [4096, 256], P(('local', 'node'))
- grad_down: float32 [4096, 256], P(('local', 'node'))
All inputs are finite; a program needn't handle non-finite values.
Results may differ from a plain program's by a relative error of at most 0.0075.
Values sent between devices are 32-bit elements; how exact they have to be, the bound alone decides.
A program may use at most 128 MiB of HBM per device.

v0:
```python
import jax
import jax.numpy as jnp
from jax import lax
from jax.sharding import PartitionSpec as P

QBLOCK = 128


def gelu_tanh(values):
    return jax.nn.gelu(values, approximate=True)


def quantize(values):
    blocks = values.reshape(values.shape[:-1] + (values.shape[-1] // QBLOCK, QBLOCK))
    scales = 2.0 * jnp.sqrt(jnp.mean(blocks * blocks, axis=-1) + 1e-06) / 7.0
    block_codes = (
        jnp.clip(blocks / scales[..., None], -7.0, 7.0).astype(jnp.bfloat16).reshape(values.shape)
    )
    return (block_codes, scales)


def restore(block_codes, scales):
    blocks = block_codes.reshape(block_codes.shape[:-1] + (scales.shape[-1], -1))
    return (blocks * scales[..., None]).reshape(block_codes.shape)


def local(tokens, out_grad, up_codes, up_scales, down_codes, down_scales):
    gathered = (
        lax.all_gather(up_codes.astype(jnp.float32), "local", axis=0, tiled=True),
        lax.all_gather(up_scales, "local", axis=0, tiled=True),
        lax.all_gather(down_codes.astype(jnp.float32), "local", axis=0, tiled=True),
        lax.all_gather(down_scales, "local", axis=0, tiled=True),
    )
    up = restore(gathered[0], gathered[1]).astype(jnp.bfloat16)
    down = restore(gathered[2], gathered[3]).astype(jnp.bfloat16)
    preact = jnp.dot(tokens, up, preferred_element_type=jnp.float32)
    activated, slope_fn = jax.vjp(gelu_tanh, preact)
    activated = activated.astype(jnp.bfloat16)
    back_grad = jnp.dot(out_grad, down, preferred_element_type=jnp.float32)
    hidden_grad = slope_fn(back_grad)[0].astype(jnp.bfloat16)
    contract_rows = (((0,), (0,)), ((), ()))
    input_grad = lax.dot_general(
        hidden_grad, up, (((1,), (1,)), ((), ())), preferred_element_type=jnp.float32
    ).astype(jnp.bfloat16)
    first = lax.dot_general(tokens, hidden_grad, contract_rows, preferred_element_type=jnp.float32)
    second = lax.dot_general(out_grad, activated, contract_rows, preferred_element_type=jnp.float32)
    block_codes, scales = quantize(jnp.stack([first, second]))
    wide_codes = block_codes.astype(jnp.float32)
    devices_all = lax.axis_size("node") * lax.axis_size("local")
    received = (
        lax.all_to_all(wide_codes[None], "local", split_axis=2, concat_axis=0, tiled=True),
        lax.all_to_all(scales[None], "local", split_axis=2, concat_axis=0, tiled=True),
    )
    summed = jnp.sum(restore(received[0], received[1]), axis=0)
    node_codes, node_scales = quantize(summed)
    owned = (
        lax.all_to_all(
            node_codes.astype(jnp.float32)[None], "node", split_axis=2, concat_axis=0, tiled=True
        ),
        lax.all_to_all(node_scales[None], "node", split_axis=2, concat_axis=0, tiled=True),
    )
    reduced = jnp.sum(restore(owned[0], owned[1]), axis=0) / devices_all
    return (input_grad, reduced[0], reduced[1])


def solution(mesh):
    placed = (
        P(("node", "local"), None),
        P(("node", "local"), None),
        P("local", None),
        P("local", None),
        P("local", None),
        P("local", None),
    )
    return jax.shard_map(
        local,
        mesh=mesh,
        in_specs=placed,
        out_specs=(
            P(("node", "local"), None),
            P(("local", "node"), None),
            P(("local", "node"), None),
        ),
        check_vma=False,
    )
```

profile of v0, /device:TPU:13, one launch (start us, length us, event | category | flops | bytes accessed | tf_op | source)
XLA Modules:
  0.0 463.4 jit_solution(4731385188587631123)
XLA Ops:
  20.9 47.1 %all-gather.5.cloned.1.call-done = f32[4096,256]{1,0:T(8,128)} async-done(((f32[2048,256]{1,0:T(8,128)}), f32[4096,256]{1,0:T(8,128)}) %all-gather.5.cloned.1.call-update) | async-done | bytes 4194320 | tf_op jit(solution)/shard_map/all_gather | solution.py:29
  68.0 9.4 %mul.108 = f32[4096,2,128]{2,1,0:T(2,128)S(1)} broadcast(f32[4096,2]{1,0:T(8,128)S(1)} %copy.20), dimensions={0,1} | broadcast | bytes 4227072 | tf_op jit(solution)/shard_map/mul | solution.py:24
  82.9 43.6 %all-gather.3.cloned.1.call-done = f32[4096,256]{1,0:T(8,128)} async-done(((f32[2048,256]{1,0:T(8,128)}), f32[4096,256]{1,0:T(8,128)}) %all-gather.3.cloned.1.call-update) | async-done | bytes 4194320 | tf_op jit(solution)/shard_map/all_gather | solution.py:31
  126.5 8.7 %mul.105 = f32[4096,2,128]{2,1,0:T(2,128)S(1)} broadcast(f32[4096,2]{1,0:T(8,128)} %copy.19), dimensions={0,1} | broadcast | bytes 4227072 | tf_op jit(solution)/shard_map/mul | solution.py:24
  140.9 4.4 copy.23
  145.2 8.1 %reshape.177 = f32[2,1,8192]{2,1,0:T(1,128)} reshape(f32[4096,1,2,2]{3,2,1,0:T(2,128)} %bitcast.101) | data formatting | bytes 131072
  156.7 6.3 %fusion.4 = f32[1,2,4096,256]{2,3,1,0:T(8,128)} fusion(f32[1,1,4096,256]{2,3,1,0:T(8,128)} %bitcast.94, f32[1,1,4096,256]{2,3,1,0:T(8,128)} %bitcast.97, f32[2,4096,2]{1,2,0:T(2,128)S(1)} %get-tuple-element.5), kind=kLoop, calls=%fused_computation.8 | loop fusion | flops 10485760 | bytes 16842752 | tf_op jit(solution)/shard_map/convert_element_type | solution.py:48
  162.9 13.1 %copy.21 = f32[1,2,4096,256]{3,1,0,2:T(2,128)} copy(f32[1,2,4096,256]{2,3,1,0:T(8,128)} %fusion.4) | data formatting | bytes 16777216 | tf_op jit(solution)/shard_map/convert_element_type | solution.py:48
  176.1 7.1 %all-to-all-start = ((f32[1,2,4096,256]{3,1,0,2:T(2,128)}), f32[1,2,4096,256]{3,1,0,2:T(2,128)}, u32[]{:S(2)}, u32[]{:S(2)}) async-start(f32[1,2,4096,256]{3,1,0,2:T(2,128)} %copy.21), calls=%async_computation | async-start | bytes 16777216 | tf_op jit(solution)/shard_map/all_to_all | solution.py:51
  184.5 8.3 %reshape.178 = f32[4096,1,2,2]{3,2,1,0:T(2,128)} reshape(f32[2,8192]{1,0:T(2,128)S(1)} %reduce) | data formatting | bytes 131072
  192.9 5.2 %copy.24 = f32[2,2,2048,2]{2,0,3,1:T(2,128)S(1)} copy(f32[2,2,2048,2]{3,1,2,0:T(2,128)} %bitcast.102) | data formatting | bytes 131072 | tf_op jit(solution)/shard_map/mul | solution.py:24
  198.1 76.7 %all-to-all-done = f32[1,2,4096,256]{3,1,0,2:T(2,128)} async-done(((f32[1,2,4096,256]{3,1,0,2:T(2,128)}), f32[1,2,4096,256]{3,1,0,2:T(2,128)}, u32[]{:S(2)}, u32[]{:S(2)}) %all-to-all-start) | async-done | bytes 8388640 | tf_op jit(solution)/shard_map/all_to_all | solution.py:51
  274.8 20.9 %copy.22 = f32[1,2,2,2048,256]{3,2,4,1,0:T(2,128)} copy(f32[1,2,2,2048,256]{4,1,3,2,0:T(2,128)} %bitcast.9) | data formatting | bytes 16777216 | tf_op jit(solution)/shard_map/all_to_all | solution.py:51
  295.6 7.5 %mul.128 = f32[2,2,2048,2,128]{2,0,4,3,1:T(2,128)} broadcast(f32[2,2,2048,2]{2,0,3,1:T(2,128)S(1)} %copy.24), dimensions={0,1,2,3} | broadcast | bytes 8454144 | tf_op jit(solution)/shard_map/mul | solution.py:24
  303.1 17.2 %fusion.3 = f32[2,2048,256]{1,2,0:T(8,128)S(1)} fusion(f32[2,2,2048,256]{2,0,3,1:T(2,128)} %bitcast.98, f32[1,2,2,2048,256]{3,2,4,1,0:T(2,128)} %copy.22), kind=kLoop, calls=%fused_computation.6 | loop fusion | flops 3145728 | bytes 20971520 | tf_op jit(solution)/shard_map/reduce_sum | solution.py:54
  325.2 5.2 %reshape.179 = f32[16,1,512]{2,1,0:T(1,128)} reshape(f32[2048,1,2,2]{3,2,1,0:T(2,128)} %bitcast.104) | data formatting | bytes 65536
  330.3 7.4 %all-to-all-start.3 = ((f32[16,1,512]{2,1,0:T(1,128)}), f32[16,1,512]{2,1,0:T(1,128)S(1)}, u32[]{:S(2)}, u32[]{:S(2)}) async-start(f32[16,1,512]{2,1,0:T(1,128)} %reshape.179), calls=%async_computation.3 | async-start | bytes 65536 | tf_op jit(solution)/shard_map/all_to_all | solution.py:60
  337.7 4.9 %fusion.9 = f32[1,2,2048,256]{2,3,1,0:T(8,128)} fusion(f32[2,2048,256]{1,2,0:T(8,128)} %copy-done.2, f32[2,2048,2]{1,2,0:T(2,128)S(1)} %get-tuple-element.8), kind=kLoop, calls=%fused_computation.18 | loop fusion | flops 4194304 | bytes 8421376 | tf_op jit(solution)/shard_map/convert_element_type | solution.py:58
  342.6 7.2 %copy.25 = f32[1,2,2048,256]{3,1,0,2:T(2,128)} copy(f32[1,2,2048,256]{2,3,1,0:T(8,128)} %fusion.9) | data formatting | bytes 8388608 | tf_op jit(solution)/shard_map/convert_element_type | solution.py:58
  349.8 6.0 %all-to-all-start.2 = ((f32[1,2,2048,256]{3,1,0,2:T(2,128)}), f32[1,2,2048,256]{3,1,0,2:T(2,128)}, u32[]{:S(2)}, u32[]{:S(2)}) async-start(f32[1,2,2048,256]{3,1,0,2:T(2,128)} %copy.25), calls=%async_computation.2 | async-start | bytes 8388608 | tf_op jit(solution)/shard_map/all_to_all | solution.py:57
  361.7 6.3 %mul.134 = f32[16,2,128,2,128]{4,3,1,2,0:T(2,128)} broadcast(f32[16,2,128,2]{3,1,2,0:T(2,128)S(1)} %bitcast.103), dimensions={0,1,2,3} | broadcast | bytes 4227072 | tf_op jit(solution)/shard_map/mul | solution.py:24
  368.0 7.6 %mul.135 = f32[16,2,128,256]{3,1,2,0:T(2,128)} reshape(f32[16,2,128,2,128]{4,3,1,2,0:T(2,128)} %mul.134) | data formatting | bytes 8388608 | tf_op jit(solution)/shard_map/mul | solution.py:24
  375.6 72.8 %all-to-all-done.2 = f32[1,2,2048,256]{3,1,0,2:T(2,128)} async-done(((f32[1,2,2048,256]{3,1,0,2:T(2,128)}), f32[1,2,2048,256]{3,1,0,2:T(2,128)}, u32[]{:S(2)}, u32[]{:S(2)}) %all-to-all-start.2) | async-done | bytes 4194336 | tf_op jit(solution)/shard_map/all_to_all | solution.py:57
  448.3 7.1 %multiply_reduce_fusion = f32[2,128,256]{2,0,1:T(2,128)S(1)} fusion(f32[16,2,128,256]{3,1,2,0:T(2,128)} %bitcast.22, f32[16,2,128,256]{3,1,2,0:T(2,128)} %mul.135), kind=kLoop, calls=%fused_computation.17 | loop fusion | flops 2031616 | bytes 8650752 | tf_op jit(solution)/shard_map/reduce_sum | solution.py:62
  (59 shorter events, 41.0 us)
Async XLA Ops:
  7.2 73.0 %copy-start = (bf16[160,4096]{1,0:T(8,128)(2,1)S(1)}, bf16[160,4096]{1,0:T(8,128)(2,1)}, u32[]{:S(2)}) copy-start(bf16[160,4096]{1,0:T(8,128)(2,1)} %param.7) | copy-start | bytes 3932164
  7.2 3.1 copy-start.11
  7.2 60.8 %all-gather.5.cloned.1.call-start = ((), (), s32[]{:S(2)}) async-start(), calls=%async_computation.5 | async-start | bytes 6291456 | tf_op jit(solution)/shard_map/all_gather | solution.py:29
  10.1 1.6 copy-start.12
  10.2 6.8 %copy-start.13 = (f32[2048,2]{0,1:T(2,128)S(1)}, f32[2048,2]{0,1:T(2,128)}, u32[]{:S(2)}) copy-start(f32[2048,2]{0,1:T(2,128)} %param.9) | copy-start | bytes 49156
  10.2 116.3 %all-gather.3.cloned.1.call-start = ((), (), s32[]{:S(2)}) async-start(), calls=%async_computation.4 | async-start | bytes 6291456 | tf_op jit(solution)/shard_map/all_gather | solution.py:31
  68.0 9.4 %copy-start.8 = (f32[4096,256]{1,0:T(8,128)S(1)}, f32[4096,256]{1,0:T(8,128)}, u32[]{:S(2)}) copy-start(f32[4096,256]{1,0:T(8,128)} %all-gather.5.cloned.1.call-done) | copy-start | bytes 12582916
  77.4 1.5 copy-start.5
  79.5 0.7 copy-start.9
  126.5 8.7 %copy-start.7 = (f32[4096,256]{1,0:T(8,128)S(1)}, f32[4096,256]{1,0:T(8,128)}, u32[]{:S(2)}) copy-start(f32[4096,256]{1,0:T(8,128)} %all-gather.3.cloned.1.call-done) | copy-start | bytes 12582916
  126.5 8.7 %copy-start.10 = (f32[160,256]{1,0:T(8,128)S(1)}, f32[160,256]{1,0:T(8,128)}, u32[]{:S(2)}) copy-start(f32[160,256]{1,0:T(8,128)} %copy-done.9) | copy-start | bytes 491524
  135.2 1.3 copy-start.6
  136.5 3.5 copy-start.3
  137.2 3.5 copy-start.4
  153.3 22.7 %all-to-all-start.1 = ((f32[2,1,8192]{2,1,0:T(1,128)}), f32[2,1,8192]{2,1,0:T(1,128)S(1)}, u32[]{:S(2)}, u32[]{:S(2)}) async-start(f32[2,1,8192]{2,1,0:T(1,128)} %reshape.177), calls=%async_computation.1 | async-start | bytes 131072 | tf_op jit(solution)/shard_map/all_to_all | solution.py:52
  176.1 98.7 %all-to-all-start = ((f32[1,2,4096,256]{3,1,0,2:T(2,128)}), f32[1,2,4096,256]{3,1,0,2:T(2,128)}, u32[]{:S(2)}, u32[]{:S(2)}) async-start(f32[1,2,4096,256]{3,1,0,2:T(2,128)} %copy.21), calls=%async_computation | async-start | bytes 16777216 | tf_op jit(solution)/shard_map/all_to_all | solution.py:51
  320.3 1.9 copy-start.2
  330.3 19.5 %all-to-all-start.3 = ((f32[16,1,512]{2,1,0:T(1,128)}), f32[16,1,512]{2,1,0:T(1,128)S(1)}, u32[]{:S(2)}, u32[]{:S(2)}) async-start(f32[16,1,512]{2,1,0:T(1,128)} %reshape.179), calls=%async_computation.3 | async-start | bytes 65536 | tf_op jit(solution)/shard_map/all_to_all | solution.py:60
  349.8 98.5 %all-to-all-start.2 = ((f32[1,2,2048,256]{3,1,0,2:T(2,128)}), f32[1,2,2048,256]{3,1,0,2:T(2,128)}, u32[]{:S(2)}, u32[]{:S(2)}) async-start(f32[1,2,2048,256]{3,1,0,2:T(2,128)} %copy.25), calls=%async_computation.2 | async-start | bytes 8388608 | tf_op jit(solution)/shard_map/all_to_all | solution.py:57
  448.3 8.2 %copy-start.1 = (bf16[160,4096]{1,0:T(8,128)(2,1)S(1)}, bf16[160,4096]{1,0:T(8,128)(2,1)}, u32[]{:S(2)}) copy-start(bf16[160,4096]{1,0:T(8,128)(2,1)} %param.7) | copy-start | bytes 3932164
Sparse Core Ops, SparseCore 0:
  10.3 57.6 all-gather.4
  69.5 56.8 all-gather.2
where the time goes:
time: 465 us; the launch traced here: 463 us
  waiting for transfers between devices  240 us (52%)
  local copies, waits for them, and re-layouts  128 us (28%)
  other arithmetic  43.8 us (9%)
  starting transfers between devices  23.9 us (5%)
  between operations  14.3 us (3%)
  matrix products  6.67 us (1%)
  blocking collectives  6.49 us (1%)
    all_to_all x1, waiting for transfers between devices, local(): lax.all_to_all(wide_codes[None], 'local', split_axis=2, concat_axis=0, ti...  76.7 us
    all_to_all x1, waiting for transfers between devices, local(): lax.all_to_all(node_codes.astype(jnp.float32)[None], 'node', split_axis=2...  72.8 us
    all_gather x1, waiting for transfers between devices, local(): lax.all_gather(up_codes.astype(jnp.float32), 'local', axis=0, tiled=True)  47.1 us
    mul x6, local copies, waits for them, and re-layouts, restore(): return (blocks * scales[..., None]).reshape(block_codes.shape)  44.7 us
    all_gather x1, waiting for transfers between devices, local(): lax.all_gather(down_codes.astype(jnp.float32), 'local', axis=0, tiled=True)  43.6 us
    unnamed x33, local copies, waits for them, and re-layouts  32.1 us
    all_to_all x1, local copies, waits for them, and re-layouts, local(): lax.all_to_all(wide_codes[None], 'local', split_axis=2, concat_axis=0, ti...  20.9 us
    reduce_sum x1, other arithmetic, local(): summed = jnp.sum(restore(received[0], received[1]), axis=0)  17.2 us
  transfers between devices with their start and end apart: 6, of which 4 were waited for; matrix products, arithmetic and copies ran while one was open for 18% of the time, Pallas kernels for 0%

commit v1 on v0

v1 whole, which is shorter than its diff:
```python
import functools

import jax
import jax.numpy as jnp
from jax import lax
from jax.experimental import pallas as pl
from jax.experimental.pallas import tpu as pltpu
from jax.sharding import PartitionSpec as P

QBLOCK = 128
MESH = pl.DeviceIdType.MESH
F32 = jnp.float32
BF16 = jnp.bfloat16


def restored(block_codes, scales):
    blocks = block_codes.astype(F32).reshape(block_codes.shape[:-1] + (scales.shape[-1], -1))
    return (blocks * scales[..., None]).reshape(block_codes.shape)


def coded(values, axis):
    power = jnp.mean(values * values, axis=axis, keepdims=True) + 1e-06
    inverse = lax.rsqrt(power)
    scale = (2.0 / 7.0) * (power * inverse)
    codes = jnp.clip(values * (3.5 * inverse), -7.0, 7.0).astype(BF16).astype(F32)
    return codes * scale


def place(index, order):
    return sum(((index // (1 << bit)) % 2) * (1 << at) for at, bit in enumerate(order))


def flipped(index, bit):
    return index + (1 - 2 * ((index // (1 << bit)) % 2)) * (1 << bit)


def kernel(
    n_node, n_local, pieces, early,
    tok, og, up, dn, own_slice, ig, gu, gd,
    xs, xr, wb, wide, hid, act, hs, hr, g, r,
    x_send, x_recv, w_send, w_recv, a_send, a_recv, h_send, h_recv, r_send, r_recv,
):
    node, loc = lax.axis_index("node"), lax.axis_index("local")
    tokens, depth = tok.shape
    hidden = up.shape[1]
    rows = depth // n_local
    owned = rows // n_node
    bits = n_node.bit_length() - 1
    flip_layout = owned % 128 == 0
    others = range(1, n_local)
    halves = hidden // QBLOCK
    piece = tokens // pieces

    def target(step):
        return lax.rem(loc + step, n_local)

    def source(step):
        return lax.rem(loc + n_local - step, n_local)

    def columns(index):
        return pl.ds(pl.multiple_of(index * rows, 128), rows)

    barrier = pltpu.get_barrier_semaphore()
    for step in others:
        pl.semaphore_signal(barrier, inc=1, device_id={"local": target(step)}, device_id_type=MESH)
    for bit in range(bits):
        pl.semaphore_signal(barrier, inc=1, device_id={"node": flipped(node, bit)}, device_id_type=MESH)
    pl.semaphore_wait(barrier, n_local - 1 + bits)

    far = [bit for bit in range(bits - 1, -1, -1)]
    near = [1] + [bit for bit in range(bits - 1, 1, -1)] + [0] if bits > 1 else far
    gather_orders = (far, near)

    w_copies = {}
    for m in range(2):
        for step in others:
            w_copies[m, step] = pltpu.make_async_remote_copy(
                src_ref=own_slice.at[m],
                dst_ref=wb.at[step - 1, m, place(node, gather_orders[m])],
                send_sem=w_send.at[step - 1, m],
                recv_sem=w_recv.at[step - 1, m],
                device_id={"local": target(step)},
                device_id_type=MESH,
            )
            w_copies[m, step].start()

    x_copies = {}
    for m in range(2):
        for step in others:
            xs[step - 1, m] = (tok, og)[m][:, columns(target(step))].astype(F32)
            for c in range(pieces):
                x_copies[m, step, c] = pltpu.make_async_remote_copy(
                    src_ref=xs.at[step - 1, m, pl.ds(c * piece, piece)],
                    dst_ref=xr.at[step - 1, m, pl.ds(c * piece, piece)],
                    send_sem=x_send.at[step - 1, m, c],
                    recv_sem=x_recv.at[step - 1, m, c],
                    device_id={"local": target(step)},
                    device_id_type=MESH,
                )
                if m == 0 or c < early:
                    x_copies[m, step, c].start()

    sums = [
        jnp.dot(tok[:, columns(loc)], up[...], preferred_element_type=F32),
        jnp.dot(og[:, columns(loc)], dn[...], preferred_element_type=F32),
    ]

    a_copies = {}
    for stage in range(bits):
        for m in range(2):
            for step in others:
                if stage == 0:
                    w_copies[m, step].wait_recv()
                else:
                    a_copies[m, step, stage - 1].wait_recv()
                size = 1 << stage
                at = place(node, gather_orders[m])
                held = wb.at[step - 1, m, pl.ds((at // size) * size, size)]
                a_copies[m, step, stage] = pltpu.make_async_remote_copy(
                    src_ref=held,
                    dst_ref=held,
                    send_sem=a_send.at[step - 1, m, stage],
                    recv_sem=a_recv.at[step - 1, m, stage],
                    device_id={"node": flipped(node, gather_orders[m][stage])},
                    device_id_type=MESH,
                )
                a_copies[m, step, stage].start()
    for m in range(2):
        for step in others:
            a_copies[m, step, bits - 1].wait_recv()
            for n in range(n_node):
                wide[step - 1, m, n * owned : (n + 1) * owned, :] = wb[
                    step - 1, m, place(n, gather_orders[m])
                ].astype(BF16)
            sums[m] += jnp.dot(
                (tok, og)[m][:, columns(source(step))],
                wide[step - 1, m],
                preferred_element_type=F32,
            )

    pre, back = sums
    root = 0.7978845608028654
    square = pre * pre
    bend = jnp.tanh(root * (pre + 0.044715 * (square * pre)))
    half = 0.5 * (1.0 + bend)
    slope = half + 0.5 * pre * (1.0 - bend * bend) * (root * (1.0 + 3.0 * 0.044715 * square))
    act[...] = (half * pre).astype(BF16)
    hid[...] = (back * slope).astype(BF16)
    hs[0] = hid[...].astype(F32)
    hs[1] = act[...].astype(F32)
    h_copies = {}
    for m in range(2):
        for step in others:
            h_copies[m, step] = pltpu.make_async_remote_copy(
                src_ref=hs.at[m],
                dst_ref=hr.at[step - 1, m],
                send_sem=h_send.at[step - 1, m],
                recv_sem=h_recv.at[step - 1, m],
                device_id={"local": target(step)},
                device_id_type=MESH,
            )
            h_copies[m, step].start()
    for c in range(early, pieces):
        for step in others:
            x_copies[1, step, c].start()

    across = (((1,), (1,)), ((), ()))
    ig[:, columns(loc)] = lax.dot_general(
        hid[...], up[...], across, preferred_element_type=F32
    ).astype(BF16)
    for step in others:
        ig[:, columns(source(step))] = lax.dot_general(
            hid[...], wide[step - 1, 0], across, preferred_element_type=F32
        ).astype(BF16)

    chunks = [(m, f) for m in range(2) for f in range(halves)]
    add_orders = [gather_orders[k % 2] for k in range(len(chunks))]
    down_rows = (((0,), (0,)), ((), ()))
    axis = 0 if flip_layout else 1
    block = max(owned, min(rows, 256))

    def term(features, values):
        pair = (features, values) if flip_layout else (values, features)
        return coded(lax.dot_general(*pair, down_rows, preferred_element_type=F32), axis)

    def compute(k):
        m, f = chunks[k]
        lanes = slice(f * QBLOCK, (f + 1) * QBLOCK)
        if f == 0:
            for step in others:
                h_copies[m, step].wait_recv()
                for c in range(pieces):
                    x_copies[m, step, c].wait_recv()
        mine = (hid, act)[m][:, lanes]
        theirs = [hr[step - 1, m, :, lanes].astype(BF16) for step in others]
        for start in range(0, rows, block):
            own = (tok, og)[m][:, pl.ds(pl.multiple_of(loc * rows + start, 128), block)]
            total = term(mine, own)
            for step in others:
                total += term(
                    theirs[step - 1], xr[step - 1, m, :, start : start + block].astype(BF16)
                )
            total = coded(total, axis)
            for sub in range(block // owned):
                at = place(start // owned + sub, add_orders[k])
                cut = slice(sub * owned, (sub + 1) * owned)
                g[k, at] = total[:, cut] if flip_layout else total[cut, :]

    region = [0] * len(chunks)
    r_copies = {}

    def start(k, stage):
        bit = add_orders[k][bits - 1 - stage]
        size = n_node >> (stage + 1)
        mine = (node // (1 << bit)) % 2
        r_copies[k, stage] = pltpu.make_async_remote_copy(
            src_ref=g.at[k, pl.ds(region[k] + (1 - mine) * size, size)],
            dst_ref=r.at[k, pl.ds(n_node - 2 * size, size)],
            send_sem=r_send.at[k, stage],
            recv_sem=r_recv.at[k, stage],
            device_id={"node": flipped(node, bit)},
            device_id_type=MESH,
        )
        r_copies[k, stage].start()
        region[k] = region[k] + mine * size

    def finish(k, stage):
        size = n_node >> (stage + 1)
        r_copies[k, stage].wait_recv()

        def add(i, carry):
            g[k, region[k] + i] += r[k, n_node - 2 * size + i]
            return carry

        lax.fori_loop(0, size, add, 0)

    def emit(k):
        m, f = chunks[k]
        value = g[k, region[k]] * (1.0 / (n_node * n_local))
        (gu, gd)[m][:, f * QBLOCK : (f + 1) * QBLOCK] = value.T if flip_layout else value

    for tick in range(len(chunks) + bits):
        for k in range(min(tick, len(chunks) - 1), -1, -1):
            stage = tick - k
            if stage > bits:
                continue
            if stage == 0:
                compute(k)
            else:
                finish(k, stage - 1)
            if stage < bits:
                start(k, stage)
            else:
                emit(k)

    for copies in (w_copies, x_copies, a_copies, h_copies, r_copies):
        for copy in copies.values():
            copy.wait_send()


def local(n_node, n_local, tokens, out_grad, up_codes, up_scales, down_codes, down_scales):
    count, depth = tokens.shape
    rows, hidden = up_codes.shape
    owned = rows // n_node
    bits = n_node.bit_length() - 1
    pieces = 4 if count % 32 == 0 else 1
    chunks = 2 * (hidden // QBLOCK)
    others = n_local - 1
    block = (QBLOCK, owned) if owned % 128 == 0 else (owned, QBLOCK)
    up = restored(up_codes, up_scales).astype(BF16)
    down = restored(down_codes, down_scales).astype(BF16)
    at = lax.axis_index("node") * owned
    own_slice = jnp.stack(
        [lax.dynamic_slice_in_dim(w, at, owned, 0).astype(F32) for w in (up, down)]
    )
    dma = pltpu.SemaphoreType.DMA
    vmem = pl.BlockSpec(memory_space=pltpu.VMEM)
    return pl.pallas_call(
        functools.partial(kernel, n_node, n_local, pieces, pieces // 2),
        out_shape=(
            jax.ShapeDtypeStruct((count, depth), BF16),
            jax.ShapeDtypeStruct((owned, hidden), F32),
            jax.ShapeDtypeStruct((owned, hidden), F32),
        ),
        in_specs=[vmem] * 5,
        out_specs=(vmem, vmem, vmem),
        scratch_shapes=[
            pltpu.VMEM((others, 2, count, rows), F32),
            pltpu.VMEM((others, 2, count, rows), F32),
            pltpu.VMEM((others, 2, n_node, owned, hidden), F32),
            pltpu.VMEM((others, 2, rows, hidden), BF16),
            pltpu.VMEM((count, hidden), BF16),
            pltpu.VMEM((count, hidden), BF16),
            pltpu.VMEM((2, count, hidden), F32),
            pltpu.VMEM((others, 2, count, hidden), F32),
            pltpu.VMEM((chunks, n_node) + block, F32),
            pltpu.VMEM((chunks, n_node) + block, F32),
            dma((others, 2, pieces)),
            dma((others, 2, pieces)),
            dma((others, 2)),
            dma((others, 2)),
            dma((others, 2, bits)),
            dma((others, 2, bits)),
            dma((others, 2)),
            dma((others, 2)),
            dma((chunks, bits)),
            dma((chunks, bits)),
        ],
        compiler_params=pltpu.CompilerParams(
            collective_id=0, has_side_effects=True, vmem_limit_bytes=56 * 1024 * 1024
        ),
    )(tokens, out_grad, up, down, own_slice)


def solution(mesh):
    placed = (
        P(("node", "local"), None),
        P(("node", "local"), None),
        P("local", None),
        P("local", None),
        P("local", None),
        P("local", None),
    )
    return jax.shard_map(
        functools.partial(local, mesh.shape["node"], mesh.shape["local"]),
        mesh=mesh,
        in_specs=placed,
        out_specs=(
            P(("node", "local"), None),
            P(("local", "node"), None),
            P(("local", "node"), None),
        ),
        check_vma=False,
    )
```

time: 465 us -> 130 us (0.28)
  the two profiles are of different devices: /device:TPU:13 before, /device:TPU:0 now
where the time goes in v1:
time: 130 us
  Pallas kernels  112 us (86%)
  local copies, waits for them, and re-layouts  15.3 us (12%)
  other arithmetic  1.59 us (1%)
    pallas_call x1, Pallas kernels, local(): pl.pallas_call(functools.partial(kernel, n_node, n_local, pieces, pieces...  112 us
    mul x2, local copies, waits for them, and re-layouts, restored(): return (blocks * scales[..., None]).reshape(block_codes.shape)  9.35 us
    unnamed x19, local copies, waits for them, and re-layouts  5.9 us

profile of v1, /device:TPU:0, one launch (start us, length us, event | category | flops | bytes accessed | tf_op | source)
XLA Modules:
  0.0 129.8 jit_solution(595519624393149416)
XLA Ops:
  0.6 0.0 copy-start.2
  0.6 1.2 copy.9
  1.8 4.7 %mul.25 = f32[2048,2,128]{2,1,0:T(2,128)S(1)} broadcast(f32[2048,2]{1,0:T(8,128)S(1)} %copy.9), dimensions={0,1} | broadcast | bytes 2113536 | tf_op jit(solution)/shard_map/mul | solution.py:18
  6.5 0.0 copy-done.2
  6.5 0.0 copy-start.6
  6.5 0.4 fusion.1.up
  6.9 0.3 copy-done.6
  7.2 0.0 copy-start
  7.2 0.4 copy.10
  7.6 4.7 %mul.28 = f32[2048,2,128]{2,1,0:T(2,128)S(1)} broadcast(f32[2048,2]{1,0:T(8,128)S(1)} %copy.10), dimensions={0,1} | broadcast | bytes 2113536 | tf_op jit(solution)/shard_map/mul | solution.py:18
  12.3 0.0 copy-done.3
  12.3 0.4 fusion.dn
  12.7 0.0 copy-start.1
  12.7 0.0 copy-done
  12.7 0.8 maximum_convert_fusion.own_slice
  13.6 0.2 copy-done.1
  13.7 112.2 %shard_map.85 = (bf16[160,4096]{1,0:T(8,128)(2,1)}, f32[128,256]{1,0:T(8,128)}, f32[128,256]{1,0:T(8,128)}) custom-call(bf16[160,4096]{1,0:T(8,128)(2,1)} %tok.1, bf16[160,4096]{1,0:T(8,128)(2,1)} %og.1, bf16[2048,256]{1,0:T(8,128)(2,1)} %copy-done, bf16[2048,256]{1,0:T(8,128)(2,1)} %copy-done.1, f32[2,128,256]{2,1,0:T(8,128)} %maximum_convert_fusion.own_slice), custom_call_target="tpu_custom_call" | custom-call | tf_op jit(solution)/shard_map/pallas_call | solution.py:278
  125.9 0.0 copy-start.5
  125.9 0.0 copy-start.4
  125.9 2.5 %copy.18 = bf16[160,4096]{1,0:T(8,128)(2,1)} copy(bf16[160,4096]{1,0:T(8,128)(2,1)} %get-tuple-element.8) | data formatting | bytes 2621440
  128.4 0.0 copy-done.5
  128.4 0.7 copy.19
  129.1 0.0 copy-done.4
  129.1 0.7 copy.20
  (2 shorter events, 0.0 us)
Async XLA Ops:
  0.6 5.9 %copy-start.2 = (bf16[2048,256]{1,0:T(8,128)(2,1)S(1)}, bf16[2048,256]{1,0:T(8,128)(2,1)}, u32[]{:S(2)}) copy-start(bf16[2048,256]{1,0:T(8,128)(2,1)} %param.8) | copy-start | bytes 3145732
  6.5 0.7 copy-start.6
  7.2 5.5 %copy-start = (bf16[2048,256]{1,0:T(8,128)(2,1)}, bf16[2048,256]{1,0:T(8,128)(2,1)S(1)}, u32[]{:S(2)}) copy-start(bf16[2048,256]{1,0:T(8,128)(2,1)S(1)} %fusion.1.up) | copy-start | bytes 3145732
  7.2 5.1 %copy-start.3 = (bf16[2048,256]{1,0:T(8,128)(2,1)S(1)}, bf16[2048,256]{1,0:T(8,128)(2,1)}, u32[]{:S(2)}) copy-start(bf16[2048,256]{1,0:T(8,128)(2,1)} %param.10) | copy-start | bytes 3145732
  12.7 1.1 copy-start.1
  125.9 2.6 %copy-start.5 = (f32[128,256]{1,0:T(8,128)S(1)}, f32[128,256]{1,0:T(8,128)}, u32[]{:S(2)}) copy-start(f32[128,256]{1,0:T(8,128)} %get-tuple-element.9) | copy-start | bytes 393220
  125.9 3.2 %copy-start.4 = (f32[128,256]{1,0:T(8,128)S(1)}, f32[128,256]{1,0:T(8,128)}, u32[]{:S(2)}) copy-start(f32[128,256]{1,0:T(8,128)} %get-tuple-element.10) | copy-start | bytes 393220

commit v2 on v1

--- a/solution.py
+++ b/solution.py
@@ -13,11 +13,6 @@
 BF16 = jnp.bfloat16
 
 
-def restored(block_codes, scales):
-    blocks = block_codes.astype(F32).reshape(block_codes.shape[:-1] + (scales.shape[-1], -1))
-    return (blocks * scales[..., None]).reshape(block_codes.shape)
-
-
 def coded(values, axis):
     power = jnp.mean(values * values, axis=axis, keepdims=True) + 1e-06
     inverse = lax.rsqrt(power)
@@ -26,6 +21,15 @@
     return codes * scale
 
 
+def paired(first, second):
+    left = lax.broadcasted_iota(jnp.int32, first.shape, 1) < QBLOCK // 2
+    turn = QBLOCK // 2
+    return (
+        jnp.where(left, first, pltpu.roll(second, turn, 1)),
+        jnp.where(left, pltpu.roll(first, turn, 1), second),
+    )
+
+
 def place(index, order):
     return sum(((index // (1 << bit)) % 2) * (1 << at) for at, bit in enumerate(order))
 
@@ -35,18 +39,19 @@
 
 
 def kernel(
-    n_node, n_local, pieces, early,
-    tok, og, up, dn, own_slice, ig, gu, gd,
-    xs, xr, wb, wide, hid, act, hs, hr, g, r,
+    n_node, n_local, paired_rows, pieces,
+    tok, og, up_codes, up_scales, dn_codes, dn_scales, ig, gu, gd,
+    xs, xr, xo, wf, wn, wb, wide, hid, act, hs, hr, g, r,
     x_send, x_recv, w_send, w_recv, a_send, a_recv, h_send, h_recv, r_send, r_recv,
 ):
     node, loc = lax.axis_index("node"), lax.axis_index("local")
     tokens, depth = tok.shape
-    hidden = up.shape[1]
+    hidden = up_codes.shape[1]
+    up, dn = wn.at[0], wn.at[1]
     rows = depth // n_local
     owned = rows // n_node
     bits = n_node.bit_length() - 1
-    flip_layout = owned % 128 == 0
+    parts = 2 if paired_rows else 1
     others = range(1, n_local)
     halves = hidden // QBLOCK
     piece = tokens // pieces
@@ -71,11 +76,61 @@
     near = [1] + [bit for bit in range(bits - 1, 1, -1)] + [0] if bits > 1 else far
     gather_orders = (far, near)
 
+    def stage_columns(values, m, index, store):
+        if not paired_rows:
+            store(0, slice(0, rows), values[:, columns(index)].astype(F32))
+            return
+        for pair in range(n_node // 2):
+            begin = index * rows + pair * 2 * owned
+            both = values[:, pl.ds(pl.multiple_of(begin, 128), 2 * owned)].astype(F32)
+            cut = slice(pair * owned, (pair + 1) * owned)
+            for part, tile in enumerate(paired(both[:, :owned], both[:, owned:])):
+                store(part, cut, tile)
+
+    x_copies = {}
+    for m in range(2):
+        for step in others:
+            for part in range(parts):
+                for c in range(pieces):
+                    x_copies[m, step, part, c] = pltpu.make_async_remote_copy(
+                        src_ref=xs.at[step - 1, m, part, pl.ds(c * piece, piece)],
+                        dst_ref=xr.at[step - 1, m, part, pl.ds(c * piece, piece)],
+                        send_sem=x_send.at[step - 1, m, part, c],
+                        recv_sem=x_recv.at[step - 1, m, part, c],
+                        device_id={"local": target(step)},
+                        device_id_type=MESH,
+                    )
+
+    def send_columns(m, part, c):
+        for step in others:
+            x_copies[m, step, part, c].start()
+
+    def stage_sends(m):
+        for step in others:
+
+            def store(part, cut, tile):
+                xs[step - 1, m, part, :, cut] = tile
+
+            stage_columns((tok, og)[m], m, target(step), store)
+
+    stage_sends(0)
+    send_columns(0, 0, 0)
+
+    for m, (codes, scales) in enumerate(((up_codes, up_scales), (dn_codes, dn_scales))):
+        for begin in range(0, rows, QBLOCK):
+            down_cut = slice(begin, begin + QBLOCK)
+            for f in range(halves):
+                lanes = slice(f * QBLOCK, (f + 1) * QBLOCK)
+                wide_scales = jnp.broadcast_to(scales[f : f + 1, down_cut], (QBLOCK, QBLOCK)).T
+                value = (codes[down_cut, lanes].astype(F32) * wide_scales).astype(BF16)
+                wn[m, down_cut, lanes] = value
+                wf[m, down_cut, lanes] = value.astype(F32)
+
     w_copies = {}
     for m in range(2):
         for step in others:
             w_copies[m, step] = pltpu.make_async_remote_copy(
-                src_ref=own_slice.at[m],
+                src_ref=wf.at[m, pl.ds(pl.multiple_of(node * owned, 8), owned)],
                 dst_ref=wb.at[step - 1, m, place(node, gather_orders[m])],
                 send_sem=w_send.at[step - 1, m],
                 recv_sem=w_recv.at[step - 1, m],
@@ -84,21 +139,22 @@
             )
             w_copies[m, step].start()
 
-    x_copies = {}
-    for m in range(2):
-        for step in others:
-            xs[step - 1, m] = (tok, og)[m][:, columns(target(step))].astype(F32)
-            for c in range(pieces):
-                x_copies[m, step, c] = pltpu.make_async_remote_copy(
-                    src_ref=xs.at[step - 1, m, pl.ds(c * piece, piece)],
-                    dst_ref=xr.at[step - 1, m, pl.ds(c * piece, piece)],
-                    send_sem=x_send.at[step - 1, m, c],
-                    recv_sem=x_recv.at[step - 1, m, c],
-                    device_id={"local": target(step)},
-                    device_id_type=MESH,
-                )
-                if m == 0 or c < early:
-                    x_copies[m, step, c].start()
+    queue = [(m, part, c) for m in range(2) for part in range(parts) for c in range(pieces)][1:]
+    early = len(queue) - len(queue) // 2
+    for m, part, c in queue[:early]:
+        if m == 0:
+            send_columns(m, part, c)
+    stage_sends(1)
+    for m, part, c in queue[:early]:
+        if m == 1:
+            send_columns(m, part, c)
+    if paired_rows:
+        for m in range(2):
+
+            def keep(part, cut, tile):
+                xo[m, part, :, cut] = tile.astype(BF16)
+
+            stage_columns((tok, og)[m], m, loc, keep)
 
     sums = [
         jnp.dot(tok[:, columns(loc)], up[...], preferred_element_type=F32),
@@ -160,9 +216,8 @@
                 device_id_type=MESH,
             )
             h_copies[m, step].start()
-    for c in range(early, pieces):
-        for step in others:
-            x_copies[1, step, c].start()
+    for m, part, c in queue[early:]:
+        send_columns(m, part, c)
 
     across = (((1,), (1,)), ((), ()))
     ig[:, columns(loc)] = lax.dot_general(
@@ -173,38 +228,50 @@
             hid[...], wide[step - 1, 0], across, preferred_element_type=F32
         ).astype(BF16)
 
-    chunks = [(m, f) for m in range(2) for f in range(halves)]
+    chunks = [(m, f) for m in range(2) for f in range(2 if paired_rows else halves)]
     add_orders = [gather_orders[k % 2] for k in range(len(chunks))]
     down_rows = (((0,), (0,)), ((), ()))
-    axis = 0 if flip_layout else 1
-    block = max(owned, min(rows, 256))
+    axis = 0 if paired_rows else 1
+    width = rows // parts
+    block = min(width, 256)
 
     def term(features, values):
-        pair = (features, values) if flip_layout else (values, features)
+        pair = (features, values) if paired_rows else (values, features)
         return coded(lax.dot_general(*pair, down_rows, preferred_element_type=F32), axis)
 
     def compute(k):
         m, f = chunks[k]
-        lanes = slice(f * QBLOCK, (f + 1) * QBLOCK)
-        if f == 0:
-            for step in others:
+        part = f if paired_rows else 0
+        for step in others:
+            if f == 0:
                 h_copies[m, step].wait_recv()
+            if paired_rows or f == 0:
                 for c in range(pieces):
-                    x_copies[m, step, c].wait_recv()
-        mine = (hid, act)[m][:, lanes]
-        theirs = [hr[step - 1, m, :, lanes].astype(BF16) for step in others]
-        for start in range(0, rows, block):
-            own = (tok, og)[m][:, pl.ds(pl.multiple_of(loc * rows + start, 128), block)]
-            total = term(mine, own)
-            for step in others:
-                total += term(
-                    theirs[step - 1], xr[step - 1, m, :, start : start + block].astype(BF16)
-                )
-            total = coded(total, axis)
-            for sub in range(block // owned):
-                at = place(start // owned + sub, add_orders[k])
-                cut = slice(sub * owned, (sub + 1) * owned)
-                g[k, at] = total[:, cut] if flip_layout else total[cut, :]
+                    x_copies[m, step, part, c].wait_recv()
+        for start in range(0, width, block):
+            cut = slice(start, start + block)
+            if paired_rows:
+                own = xo[m, part, :, cut]
+            else:
+                own = (tok, og)[m][:, pl.ds(pl.multiple_of(loc * rows + start, 128), block)]
+            received = [xr[step - 1, m, part, :, cut].astype(BF16) for step in others]
+            totals = []
+            for at in range(halves) if paired_rows else (f,):
+                lanes = slice(at * QBLOCK, (at + 1) * QBLOCK)
+                total = term((hid, act)[m][:, lanes], own)
+                for step in others:
+                    total += term(hr[step - 1, m, :, lanes].astype(BF16), received[step - 1])
+                totals.append(coded(total, axis))
+            if paired_rows:
+                for tile in range(block // QBLOCK):
+                    lanes = slice(tile * QBLOCK, (tile + 1) * QBLOCK)
+                    owner = 2 * (start // QBLOCK + tile)
+                    for sub, value in enumerate(paired(totals[0][:, lanes], totals[1][:, lanes])):
+                        g[k, place(owner + sub, add_orders[k])] = value
+            else:
+                for sub in range(block // owned):
+                    at = place(start // owned + sub, add_orders[k])
+                    g[k, at] = totals[0][sub * owned : (sub + 1) * owned, :]
 
     region = [0] * len(chunks)
     r_copies = {}
@@ -237,7 +304,15 @@
     def emit(k):
         m, f = chunks[k]
         value = g[k, region[k]] * (1.0 / (n_node * n_local))
-        (gu, gd)[m][:, f * QBLOCK : (f + 1) * QBLOCK] = value.T if flip_layout else value
+        if paired_rows:
+            turned = value.T
+            size = owned // 2
+            for at in range(2):
+                (gu, gd)[m][f * size : (f + 1) * size, at * QBLOCK : (at + 1) * QBLOCK] = turned[
+                    at * size : (at + 1) * size
+                ]
+        else:
+            (gu, gd)[m][:, f * QBLOCK : (f + 1) * QBLOCK] = value
 
     for tick in range(len(chunks) + bits):
         for k in range(min(tick, len(chunks) - 1), -1, -1):
@@ -263,30 +338,29 @@
     rows, hidden = up_codes.shape
     owned = rows // n_node
     bits = n_node.bit_length() - 1
-    pieces = 4 if count % 32 == 0 else 1
-    chunks = 2 * (hidden // QBLOCK)
+    pieces = 2 if count % 16 == 0 else 1
+    paired_rows = owned == QBLOCK and hidden == 2 * QBLOCK and n_node % 2 == 0
+    parts = 2 if paired_rows else 1
+    chunks = 4 if paired_rows else 2 * (hidden // QBLOCK)
     others = n_local - 1
-    block = (QBLOCK, owned) if owned % 128 == 0 else (owned, QBLOCK)
-    up = restored(up_codes, up_scales).astype(BF16)
-    down = restored(down_codes, down_scales).astype(BF16)
-    at = lax.axis_index("node") * owned
-    own_slice = jnp.stack(
-        [lax.dynamic_slice_in_dim(w, at, owned, 0).astype(F32) for w in (up, down)]
-    )
+    block = (owned, QBLOCK)
     dma = pltpu.SemaphoreType.DMA
     vmem = pl.BlockSpec(memory_space=pltpu.VMEM)
     return pl.pallas_call(
-        functools.partial(kernel, n_node, n_local, pieces, pieces // 2),
+        functools.partial(kernel, n_node, n_local, paired_rows, pieces),
         out_shape=(
             jax.ShapeDtypeStruct((count, depth), BF16),
             jax.ShapeDtypeStruct((owned, hidden), F32),
             jax.ShapeDtypeStruct((owned, hidden), F32),
         ),
-        in_specs=[vmem] * 5,
+        in_specs=[vmem] * 6,
         out_specs=(vmem, vmem, vmem),
         scratch_shapes=[
-            pltpu.VMEM((others, 2, count, rows), F32),
-            pltpu.VMEM((others, 2, count, rows), F32),
+            pltpu.VMEM((others, 2, parts, count, rows // parts), F32),
+            pltpu.VMEM((others, 2, parts, count, rows // parts), F32),
+            pltpu.VMEM((2, parts, count, rows // parts), BF16),
+            pltpu.VMEM((2, rows, hidden), F32),
+            pltpu.VMEM((2, rows, hidden), BF16),
             pltpu.VMEM((others, 2, n_node, owned, hidden), F32),
             pltpu.VMEM((others, 2, rows, hidden), BF16),
             pltpu.VMEM((count, hidden), BF16),
@@ -295,8 +369,8 @@
             pltpu.VMEM((others, 2, count, hidden), F32),
             pltpu.VMEM((chunks, n_node) + block, F32),
             pltpu.VMEM((chunks, n_node) + block, F32),
-            dma((others, 2, pieces)),
-            dma((others, 2, pieces)),
+            dma((others, 2, parts, pieces)),
+            dma((others, 2, parts, pieces)),
             dma((others, 2)),
             dma((others, 2)),
             dma((others, 2, bits)),
@@ -309,7 +383,7 @@
         compiler_params=pltpu.CompilerParams(
             collective_id=0, has_side_effects=True, vmem_limit_bytes=56 * 1024 * 1024
         ),
-    )(tokens, out_grad, up, down, own_slice)
+    )(tokens, out_grad, up_codes, up_scales.T, down_codes, down_scales.T)
 
 
 def solution(mesh):

time: 130 us -> 111 us (0.85)
  local copies, waits for them, and re-layouts: 15.3 us -> 3.85 us
  Pallas kernels: 112 us -> 106 us
  other arithmetic: 1.59 us -> 0 us
    mul x2 -> x0, local copies, waits for them, and re-layouts: 9.35 us -> none  [restored(): return (blocks * scales[..., None]).reshape(block_codes.shape)]
    pallas_call x1, Pallas kernels: 112 us -> 106 us  [local(): pl.pallas_call(functools.partial(kernel, n_node, n_local, paired_rows, pi...]
    unnamed x19 -> x7, local copies, waits for them, and re-layouts: 5.9 us -> 3.85 us
where the time goes in v2:
time: 111 us
  Pallas kernels  106 us (95%)
  local copies, waits for them, and re-layouts  3.85 us (3%)
    pallas_call x1, Pallas kernels, local(): pl.pallas_call(functools.partial(kernel, n_node, n_local, paired_rows, pi...  106 us
    unnamed x7, local copies, waits for them, and re-layouts  3.85 us

profile of v2, /device:TPU:0, one launch (start us, length us, event | category | flops | bytes accessed | tf_op | source)
XLA Modules:
  0.0 110.8 jit_solution(430377706924735749)
XLA Ops:
  0.6 106.3 %shard_map.85 = (bf16[160,4096]{1,0:T(8,128)(2,1)}, f32[128,256]{1,0:T(8,128)}, f32[128,256]{1,0:T(8,128)}) custom-call(bf16[160,4096]{1,0:T(8,128)(2,1)} %tok.1, bf16[160,4096]{1,0:T(8,128)(2,1)} %og.1, bf16[2048,256]{1,0:T(8,128)(2,1)} %up_codes.1, f32[2,2048]{1,0:T(2,128)} %bitcast.2, bf16[2048,256]{1,0:T(8,128)(2,1)} %dn_codes.1, f32[2,2048]{1,0:T(2,128)} %bitcast.3), custom_call_target="tpu_custom_call" | custom-call | tf_op jit(solution)/shard_map/pallas_call | solution.py:349
  107.0 0.0 copy-start.1
  107.0 0.0 copy-start
  107.0 2.5 %copy.12 = bf16[160,4096]{1,0:T(8,128)(2,1)} copy(bf16[160,4096]{1,0:T(8,128)(2,1)} %get-tuple-element.6) | data formatting | bytes 2621440
  109.5 0.0 copy-done.1
  109.5 0.7 copy.13
  110.2 0.0 copy-done
  110.2 0.7 copy.14
Async XLA Ops:
  107.0 2.6 %copy-start.1 = (f32[128,256]{1,0:T(8,128)S(1)}, f32[128,256]{1,0:T(8,128)}, u32[]{:S(2)}) copy-start(f32[128,256]{1,0:T(8,128)} %get-tuple-element.7) | copy-start | bytes 393220
  107.0 3.2 %copy-start = (f32[128,256]{1,0:T(8,128)S(1)}, f32[128,256]{1,0:T(8,128)}, u32[]{:S(2)}) copy-start(f32[128,256]{1,0:T(8,128)} %get-tuple-element.8) | copy-start | bytes 393220

commit v3 on v2

--- a/solution.py
+++ b/solution.py
@@ -140,7 +140,7 @@
             w_copies[m, step].start()
 
     queue = [(m, part, c) for m in range(2) for part in range(parts) for c in range(pieces)][1:]
-    early = len(queue) - len(queue) // 2
+    early = 2 * len(queue) // 3
     for m, part, c in queue[:early]:
         if m == 0:
             send_columns(m, part, c)
@@ -229,7 +229,9 @@
         ).astype(BF16)
 
     chunks = [(m, f) for m in range(2) for f in range(2 if paired_rows else halves)]
-    add_orders = [gather_orders[k % 2] for k in range(len(chunks))]
+    units = parts
+    add_orders = [gather_orders[u % 2] for u in range(units * len(chunks))]
+    height = g.shape[2]
     down_rows = (((0,), (0,)), ((), ()))
     axis = 0 if paired_rows else 1
     width = rows // parts
@@ -267,13 +269,15 @@
                     lanes = slice(tile * QBLOCK, (tile + 1) * QBLOCK)
                     owner = 2 * (start // QBLOCK + tile)
                     for sub, value in enumerate(paired(totals[0][:, lanes], totals[1][:, lanes])):
-                        g[k, place(owner + sub, add_orders[k])] = value
+                        for u in range(units):
+                            at = place(owner + sub, add_orders[k * units + u])
+                            g[k * units + u, at] = value[u * height : (u + 1) * height]
             else:
                 for sub in range(block // owned):
                     at = place(start // owned + sub, add_orders[k])
                     g[k, at] = totals[0][sub * owned : (sub + 1) * owned, :]
 
-    region = [0] * len(chunks)
+    region = [0] * len(add_orders)
     r_copies = {}
 
     def start(k, stage):
@@ -303,7 +307,9 @@
 
     def emit(k):
         m, f = chunks[k]
-        value = g[k, region[k]] * (1.0 / (n_node * n_local))
+        value = jnp.concatenate(
+            [g[u, region[u]] for u in range(k * units, (k + 1) * units)], axis=0
+        ) * (1.0 / (n_node * n_local))
         if paired_rows:
             turned = value.T
             size = owned // 2
@@ -314,19 +320,20 @@
         else:
             (gu, gd)[m][:, f * QBLOCK : (f + 1) * QBLOCK] = value
 
-    for tick in range(len(chunks) + bits):
-        for k in range(min(tick, len(chunks) - 1), -1, -1):
-            stage = tick - k
-            if stage > bits:
-                continue
-            if stage == 0:
-                compute(k)
-            else:
-                finish(k, stage - 1)
+    begins = [0.0, 0.4, 2.6, 7.6] if len(chunks) == 4 else list(range(len(chunks)))
+    events = sorted(
+        (begins[k] + stage, k, stage) for k in range(len(chunks)) for stage in range(bits + 1)
+    )
+    for _, k, stage in events:
+        if stage == 0:
+            compute(k)
+        for u in range(k * units, (k + 1) * units):
+            if stage > 0:
+                finish(u, stage - 1)
             if stage < bits:
-                start(k, stage)
-            else:
-                emit(k)
+                start(u, stage)
+        if stage == bits:
+            emit(k)
 
     for copies in (w_copies, x_copies, a_copies, h_copies, r_copies):
         for copy in copies.values():
@@ -338,12 +345,13 @@
     rows, hidden = up_codes.shape
     owned = rows // n_node
     bits = n_node.bit_length() - 1
-    pieces = 2 if count % 16 == 0 else 1
+    pieces = 4 if count % 32 == 0 else 1
     paired_rows = owned == QBLOCK and hidden == 2 * QBLOCK and n_node % 2 == 0
     parts = 2 if paired_rows else 1
     chunks = 4 if paired_rows else 2 * (hidden // QBLOCK)
     others = n_local - 1
-    block = (owned, QBLOCK)
+    units = parts
+    block = (owned // units, QBLOCK)
     dma = pltpu.SemaphoreType.DMA
     vmem = pl.BlockSpec(memory_space=pltpu.VMEM)
     return pl.pallas_call(
@@ -367,8 +375,8 @@
             pltpu.VMEM((count, hidden), BF16),
             pltpu.VMEM((2, count, hidden), F32),
             pltpu.VMEM((others, 2, count, hidden), F32),
-            pltpu.VMEM((chunks, n_node) + block, F32),
-            pltpu.VMEM((chunks, n_node) + block, F32),
+            pltpu.VMEM((chunks * units, n_node) + block, F32),
+            pltpu.VMEM((chunks * units, n_node) + block, F32),
             dma((others, 2, parts, pieces)),
             dma((others, 2, parts, pieces)),
             dma((others, 2)),
@@ -377,8 +385,8 @@
             dma((others, 2, bits)),
             dma((others, 2)),
             dma((others, 2)),
-            dma((chunks, bits)),
-            dma((chunks, bits)),
+            dma((chunks * units, bits)),
+            dma((chunks * units, bits)),
         ],
         compiler_params=pltpu.CompilerParams(
             collective_id=0, has_side_effects=True, vmem_limit_bytes=56 * 1024 * 1024

time: 111 us -> 111 us (level)
  no operation moved by 1% of the time
where the time goes in v3:
time: 111 us; the launch traced here: 110 us
  Pallas kernels  106 us (95%)
  local copies, waits for them, and re-layouts  3.85 us (3%)
    pallas_call x1, Pallas kernels, local(): pl.pallas_call(functools.partial(kernel, n_node, n_local, paired_rows, pi...  106 us
    unnamed x7, local copies, waits for them, and re-layouts  3.85 us

profile of v3, /device:TPU:0, one launch (start us, length us, event | category | flops | bytes accessed | tf_op | source)
XLA Modules:
  0.0 110.5 jit_solution(18031092780702295891)
XLA Ops:
  0.6 106.0 %shard_map.85 = (bf16[160,4096]{1,0:T(8,128)(2,1)}, f32[128,256]{1,0:T(8,128)}, f32[128,256]{1,0:T(8,128)}) custom-call(bf16[160,4096]{1,0:T(8,128)(2,1)} %tok.1, bf16[160,4096]{1,0:T(8,128)(2,1)} %og.1, bf16[2048,256]{1,0:T(8,128)(2,1)} %up_codes.1, f32[2,2048]{1,0:T(2,128)} %bitcast.2, bf16[2048,256]{1,0:T(8,128)(2,1)} %dn_codes.1, f32[2,2048]{1,0:T(2,128)} %bitcast.3), custom_call_target="tpu_custom_call" | custom-call | tf_op jit(solution)/shard_map/pallas_call | solution.py:357
  106.6 0.0 copy-start.1
  106.6 0.0 copy-start
  106.6 2.5 %copy.12 = bf16[160,4096]{1,0:T(8,128)(2,1)} copy(bf16[160,4096]{1,0:T(8,128)(2,1)} %get-tuple-element.6) | data formatting | bytes 2621440
  109.2 0.0 copy-done.1
  109.2 0.7 copy.13
  109.8 0.0 copy-done
  109.8 0.7 copy.14
Async XLA Ops:
  106.6 2.6 %copy-start.1 = (f32[128,256]{1,0:T(8,128)S(1)}, f32[128,256]{1,0:T(8,128)}, u32[]{:S(2)}) copy-start(f32[128,256]{1,0:T(8,128)} %get-tuple-element.7) | copy-start | bytes 393220
  106.6 3.2 %copy-start = (f32[128,256]{1,0:T(8,128)S(1)}, f32[128,256]{1,0:T(8,128)}, u32[]{:S(2)}) copy-start(f32[128,256]{1,0:T(8,128)} %get-tuple-element.8) | copy-start | bytes 393220
